TPU v7x, 8 devices: a whole 2x2x1 slice. The times are simulated.
8 devices in a mesh: data: 1 (over z), seq: 8 (over y, x, core).
Axes of the slice: x: 2, y: 2, z: 1, core: 2. Of those that a mesh axis runs over, the one named last changes fastest.
Arguments:
- tokens: bfloat16 [2, 256, 1024], P('data', 'seq')
- lengths: int32 [2], P('data')
- slot_param: bfloat16 [1024, 512], replicated
- logit_scale: float32 [], replicated
- w_in: bfloat16 [32, 1024, 4096], P('seq')
- w_out: bfloat16 [32, 4096, 1024], P('seq')
Outputs:
- output: bfloat16 [2, 256, 1024], P('data', 'seq')
All inputs are finite; a program needn't handle non-finite values.
Results may differ from a plain program's by a relative error of at most 0.0131918.
Values are sent between devices in bfloat16 or wider.
A program may use at most 1 GiB of HBM per device.

v0:
```python
import jax
import jax.numpy as jnp
from jax import lax
from jax.sharding import PartitionSpec as P

EPSILON = 1e-6
NEG_FILL = -1e30


def l2_normed(values, axis_dim):
    v32 = values.astype(jnp.float32)
    return (v32 * lax.rsqrt(jnp.sum(v32 * v32, axis=axis_dim, keepdims=True) + EPSILON)).astype(jnp.bfloat16)


def solution(mesh):
    seq_size = mesh.shape["seq"]

    def local_layer(tok_blk, len_blk, slot_param, logit_scale, w_in, w_out):
        batch_loc, tok_loc, d_model = tok_blk.shape
        n_slots = slot_param.shape[1]
        exp_loc = w_in.shape[0]
        slot_loc = n_slots // seq_size
        per_exp = slot_loc // exp_loc
        positions = lax.axis_index("seq") * tok_loc + jnp.arange(tok_loc, dtype=jnp.int32)
        tok_valid = (positions[None, :] < len_blk[:, None])[:, :, None]
        logits = logit_scale * jnp.einsum("btd,dn->btn", l2_normed(tok_blk, 2), l2_normed(slot_param, 0), preferred_element_type=jnp.float32)
        masked = jnp.where(tok_valid, logits, NEG_FILL)
        col_max = lax.pmax(jnp.max(masked, axis=1, keepdims=True), "seq")
        disp_w = jnp.exp(masked - col_max)
        col_sum = lax.psum_scatter(jnp.sum(disp_w, axis=1), "seq", scatter_dimension=1, tiled=True)
        part_sum = jnp.einsum("btn,btd->bnd", disp_w.astype(jnp.bfloat16), tok_blk, preferred_element_type=jnp.float32)
        slot_sum = lax.psum_scatter(part_sum.astype(jnp.bfloat16), "seq", scatter_dimension=1, tiled=True)
        slot_in = (slot_sum.astype(jnp.float32) / col_sum[:, :, None]).astype(jnp.bfloat16)
        slot_grp = slot_in.reshape(batch_loc, exp_loc, per_exp, d_model)
        hidden = jax.nn.gelu(jnp.einsum("besd,edf->besf", slot_grp, w_in, preferred_element_type=jnp.float32)).astype(jnp.bfloat16)
        own_out = jnp.einsum("besf,efd->besd", hidden, w_out, preferred_element_type=jnp.float32).astype(jnp.bfloat16)
        slot_out = lax.all_gather(own_out.reshape(batch_loc, slot_loc, d_model), "seq", axis=1, tiled=True)
        comb_w = jnp.exp(logits - jnp.max(logits, axis=2, keepdims=True))
        row_sum = jnp.sum(comb_w, axis=2, keepdims=True)
        tok_mixed = jnp.einsum("btn,bnd->btd", comb_w.astype(jnp.bfloat16), slot_out, preferred_element_type=jnp.float32) / row_sum
        return jnp.where(tok_valid, tok_mixed, 0.0).astype(jnp.bfloat16)

    return jax.shard_map(local_layer, mesh=mesh, in_specs=(P("data", "seq", None), P("data"), P(None, None), P(), P("seq", None, None), P("seq", None, None)), out_specs=P("data", "seq", None), check_vma=False)
```

profile of v0, /device:TPU:0, one launch (start us, length us, event | category | flops | bytes accessed | tf_op | source)
XLA Modules:
  0.0 164.1 jit_solution(15763333202683337352)
XLA Ops:
  6.5 0.0 reduce-scatter.7.cloned.1.call-start
  7.2 1.0 fusion.30
  8.3 1.5 fusion.7
  9.8 0.7 broadcast_compare_fusion
  10.5 1.8 %fusion.46 = (f32[2,32]{1,0:T(2,128)S(1)}, f32[2,512]{1,0:T(2,128)S(1)}, f32[2,32,512]{2,1,0:T(8,128)S(1)}) fusion(pred[2,32]{1,0:T(4,128)(4,1)S(1)} %broadcast_compare_fusion, bf16[1024,512]{1,0:T(8,128)(2,1)} %param.8, f32[512]{0:T(512)S(1)} %add_rsqrt_fusion, bf16[2,32,1024]{2,1,0:T(8,128)(2,1)} %param.6, f32[2,32]{1,0:T(2,128)S(1)} %add_rsqrt_fusion.1, ...), kind=kOutput, calls=%fused_computation.50 | convolution fusion | flops 69008320 | bytes 1317444 | tf_op jit(solution)/shard_map/btd,dn->btn/dot_general | solution.py:26
  12.3 25.1 %pmax.7 = f32[2,512]{1,0:T(2,128)S(1)} all-reduce(f32[2,512]{1,0:T(2,128)S(1)} %get-tuple-element.8), channel_id=1, replica_groups=mesh['data'=1,'seq'=8] {'seq'}, use_global_device_ids=true, to_apply=%region_4.5 | all-reduce | flops 1024 | bytes 8192 | tf_op jit(solution)/shard_map/pmax | solution.py:28
  37.4 0.2 fusion.35
  37.5 0.9 copy.14
  38.4 0.0 reduce-scatter.7.cloned.1.call-update
  38.4 0.0 reduce-scatter.5.cloned.1.call-start
  38.5 0.0 copy-done
  38.5 2.2 %convolution_convert_fusion = bf16[2,512,1024]{2,1,0:T(8,128)(2,1)} fusion(bf16[2,32,1024]{2,1,0:T(8,128)(2,1)S(1)} %copy-done, f32[2,32,512]{2,1,0:T(8,128)S(1)} %get-tuple-element.9, f32[2,512]{1,0:T(2,128)S(1)} %pmax.7, pred[2,32]{1,0:T(4,128)(4,1)S(1)} %broadcast_compare_fusion), kind=kOutput, calls=%fused_computation.18 | convolution fusion | flops 68255744 | bytes 2363456 | tf_op jit(solution)/shard_map/btn,btd->bnd/dot_general | solution.py:31
  40.7 0.0 reduce-scatter.5.cloned.1.call-update
  40.7 0.0 all-gather.2.cloned.1.call-start
  40.8 24.0 %reduce-scatter.7.cloned.1.call-done = f32[64,2]{1,0:T(8,128)} async-done(((f32[512,2]{1,0:T(8,128)}), f32[64,2]{1,0:T(8,128)}) %reduce-scatter.7.cloned.1.call-update) | async-done | bytes 528
  64.8 0.8 copy.15
  65.6 35.0 %reduce-scatter.5.cloned.1.call-done = bf16[2,64,1024]{2,1,0:T(8,128)(2,1)} async-done(((bf16[2,512,1024]{2,1,0:T(8,128)(2,1)}), bf16[2,64,1024]{2,1,0:T(8,128)(2,1)}) %reduce-scatter.5.cloned.1.call-update) | async-done | bytes 262160 | tf_op jit(solution)/shard_map/reduce_scatter | solution.py:32
  100.6 1.1 divide_convert_fusion
  101.6 16.6 %fusion.16 = bf16[2,4,16,4096]{3,2,0,1:T(8,128)(2,1)S(1)} fusion(bf16[4,1024,4096]{2,1,0:T(8,128)(2,1)} %param.10, bf16[2,4,16,1024]{3,2,1,0:T(8,128)(2,1)S(1)} %bitcast.36), kind=kOutput, calls=%fused_computation.17 | convolution fusion | flops 1078460416 | bytes 34865152 | tf_op jit(solution)/shard_map/besd,edf->besf/dot_general | solution.py:35
  118.3 13.6 %fusion.23 = bf16[2,4,16,1024]{3,2,0,1:T(8,128)(2,1)S(1)} fusion(bf16[2,4,16,4096]{3,2,0,1:T(8,128)(2,1)S(1)} %fusion.16, bf16[4,4096,1024]{2,1,0:T(8,128)(2,1)} %param.11), kind=kOutput, calls=%fused_computation.22 | convolution fusion | flops 1073872896 | bytes 34865152 | tf_op jit(solution)/shard_map/besf,efd->besd/dot_general | solution.py:36
  131.9 0.7 copy.11
  132.6 0.0 all-gather.2.cloned.1.call-update
  132.7 22.1 %all-gather.2.cloned.1.call-done = bf16[2,512,1024]{2,1,0:T(8,128)(2,1)} async-done(((bf16[2,64,1024]{2,1,0:T(8,128)(2,1)}), bf16[2,512,1024]{2,1,0:T(8,128)(2,1)}) %all-gather.2.cloned.1.call-update) | async-done | bytes 2097168 | tf_op jit(solution)/shard_map/all_gather | solution.py:37
  154.8 2.8 %fusion.26 = bf16[2,32,1024]{2,1,0:T(8,128)(2,1)} fusion(bf16[2,512,1024]{2,1,0:T(8,128)(2,1)} %all-gather.2.cloned.1.call-done, f32[2,32]{1,0:T(2,128)S(1)} %get-tuple-element.5, pred[2,32]{1,0:T(4,128)(4,1)S(1)} %broadcast_compare_fusion, f32[2,32,512]{2,1,0:T(8,128)S(1)} %get-tuple-element.9, f32[2,32]{1,0:T(2,128)S(1)} %get-tuple-element.7), kind=kOutput, calls=%fused_computation.23 | convolution fusion | flops 67371008 | bytes 2359872 | tf_op jit(solution)/shard_map/btn,bnd->btd/dot_general | solution.py:40
  (4 shorter events, 0.0 us)
Async XLA Ops:
  6.5 31.9 %copy-start = (bf16[2,32,1024]{2,1,0:T(8,128)(2,1)S(1)}, bf16[2,32,1024]{2,1,0:T(8,128)(2,1)}, u32[]{:S(2)}) copy-start(bf16[2,32,1024]{2,1,0:T(8,128)(2,1)} %param.6) | copy-start | bytes 393220
  6.5 58.2 %reduce-scatter.7.cloned.1.call-start = ((), (), s32[]{:S(2)}) async-start(), calls=%async_computation.4 | async-start | bytes 294912
  38.4 62.1 %reduce-scatter.5.cloned.1.call-start = ((), (), s32[]{:S(2)}) async-start(), calls=%async_computation.2 | async-start | bytes 2359296 | tf_op jit(solution)/shard_map/reduce_scatter | solution.py:32
  40.7 114.1 %all-gather.2.cloned.1.call-start = ((), (), s32[]{:S(2)}) async-start(), calls=%async_computation.3 | async-start | bytes 2359296 | tf_op jit(solution)/shard_map/all_gather | solution.py:37
Sparse Core Ops, SparseCore 0:
  38.6 26.1 reduce-scatter.6
  68.0 32.5 reduce-scatter.4
  132.8 21.9 all-gather.1
where the time goes:
time: 164 us
  waiting for transfers between devices  81.1 us (49%)
  matrix products  36.9 us (22%)
  blocking collectives  25.1 us (15%)
  between operations  13.8 us (8%)
  other arithmetic  4.52 us (3%)
  local copies, waits for them, and re-layouts  2.44 us (1%)
    reduce_scatter x1, waiting for transfers between devices, local_layer(): lax.psum_scatter(part_sum.astype(jnp.bfloat16), 'seq', scatter_dimension=...  35 us
    pmax x1, blocking collectives, local_layer(): col_max = lax.pmax(jnp.max(masked, axis=1, keepdims=True), 'seq')  25.1 us
    unnamed x4, waiting for transfers between devices  24.1 us
    all_gather x1, waiting for transfers between devices, local_layer(): lax.all_gather(own_out.reshape(batch_loc, slot_loc, d_model), 'seq', axis...  22.1 us
    dot_general x1, matrix products, local_layer(): jnp.einsum('besd,edf->besf', slot_grp, w_in, preferred_element_type=jnp.f...  16.6 us
    dot_general x1, matrix products, local_layer(): jnp.einsum('besf,efd->besd', hidden, w_out, preferred_element_type=jnp.fl...  13.6 us
  transfers between devices with their start and end apart: 3, of which 3 were waited for; matrix products, arithmetic and copies ran while one was open for 2% of the time, Pallas kernels for 0%

commit v1 on v0

v1 whole, which is shorter than its diff:
```python
import jax
import jax.numpy as jnp
from jax import lax
from jax.experimental import pallas as pl
from jax.experimental.pallas import tpu as pltpu
from jax.sharding import PartitionSpec as P

EPSILON = 1e-6
NEG_FILL = -1e30
MESH = pl.DeviceIdType.MESH
F32 = jnp.float32
BF16 = jnp.bfloat16


def row_normed(v):
    v32 = v.astype(F32)
    return (v32 * lax.rsqrt(jnp.sum(v32 * v32, axis=-1, keepdims=True) + EPSILON)).astype(BF16)


def layer_kernel(len_ref, g_ref, x_hbm, phi_hbm, w1_hbm, w2_hbm, y_ref,
                 xg, xn, phi_v, pn, pnt, xs, h_v, yg, cw, qs, w1b, w2b,
                 x_sem, phi_sem, w1_sem, w2_sem, w2l_sem,
                 sx_sem, rx_sem, sy_sem, ry_sem):
    batch, tok, d_model = y_ref.shape
    n_exp = w1_hbm.shape[0]
    ff = w1_hbm.shape[2]
    n_slots = phi_hbm.shape[1]
    all_tok = xg.shape[1]
    slots = xs.shape[1]
    per = slots // n_exp
    ring = w1b.shape[0]
    chunks = w2l_sem.shape[0]
    width = d_model // chunks

    me = lax.axis_index("seq")
    core = lax.rem(me, 2)
    chip = lax.div(me, 2)
    part = me + 1 - 2 * core
    xnb = me + 2 - 4 * lax.rem(chip, 2)
    ynb = me + 4 - 8 * lax.div(chip, 2)
    dia = xnb + ynb - me
    flip = 1 - 2 * core
    owners = (part, xnb, ynb, dia, xnb + flip, ynb + flip, dia + flip)

    barrier = pltpu.get_barrier_semaphore()
    for dev in owners[:4]:
        pl.semaphore_signal(barrier, inc=1, device_id={"seq": dev}, device_id_type=MESH)

    def tok_rows(dev):
        return pl.ds(pl.multiple_of(dev * tok, tok), tok)

    own_x = pltpu.make_async_copy(x_hbm, xg.at[:, tok_rows(me), :], x_sem)
    own_x.start()
    own_phi = pltpu.make_async_copy(phi_hbm, phi_v, phi_sem)
    own_phi.start()

    def w1_copy(e):
        return pltpu.make_async_copy(w1_hbm.at[e], w1b.at[lax.rem(e, ring)], w1_sem.at[lax.rem(e, ring)])

    def w2_copy(e):
        return pltpu.make_async_copy(w2_hbm.at[e], w2b.at[lax.rem(e, ring)], w2_sem.at[lax.rem(e, ring)])

    def w2_last(c):
        cols = pl.ds(c * width, width)
        return pltpu.make_async_copy(w2_hbm.at[n_exp - 1, :, cols], w2b.at[(n_exp - 1) % ring, :, cols], w2l_sem.at[c])

    for e in range(ring):
        w1_copy(e).start()
        w2_copy(e).start()

    def x_send(owner, rel, to, k):
        block = xg.at[:, tok_rows(owner), :]
        return pltpu.make_async_remote_copy(src_ref=block, dst_ref=block, send_sem=sx_sem.at[k],
                                            recv_sem=rx_sem.at[rel], device_id={"seq": to}, device_id_type=MESH)

    own_x.wait()
    pl.semaphore_wait(barrier, 4)
    x_sends = [x_send(me, 1, xnb, 1), x_send(me, 2, ynb, 2), x_send(me, 3, dia, 3), x_send(me, 0, part, 0)]
    for copy in x_sends:
        copy.start()

    own_phi.wait()
    for c in range(n_slots // 128):
        cols = pl.ds(c * 128, 128)
        p32 = phi_v[:, cols].astype(F32)
        pn[:, cols] = (p32 * lax.rsqrt(jnp.sum(p32 * p32, axis=0, keepdims=True) + EPSILON)).astype(BF16)
    chip_cols = pl.ds(pl.multiple_of(chip * 128, 128), 128)
    pnt[...] = pn[:, chip_cols].T
    g = g_ref[0, 0]

    def normalise(dev):
        for b in range(batch):
            xn[b, tok_rows(dev), :] = row_normed(xg[b, tok_rows(dev), :])

    normalise(me)
    for b in range(batch):
        own_l = g * jnp.dot(xn[b, tok_rows(me), :], pn[...], preferred_element_type=F32)
        c_exp = jnp.exp(own_l - jnp.max(own_l, axis=1, keepdims=True))
        cw[b] = c_exp.astype(BF16)
        qs[b] = jnp.broadcast_to(jnp.sum(c_exp, axis=1, keepdims=True), qs.shape[1:])

    def x_wait(rel):
        x_send(owners[rel], rel, part, 0).wait_recv()

    x_wait(0)
    normalise(owners[0])
    for rel in (1, 2, 3):
        x_wait(rel)
        fwd = x_send(owners[rel], rel + 3, part, rel + 3)
        fwd.start()
        x_sends.append(fwd)
        normalise(owners[rel])
    for rel in (4, 5, 6):
        x_wait(rel)
        normalise(owners[rel])

    own_pnt = pnt[pl.ds(pl.multiple_of(core * slots, slots), slots), :]
    for b in range(batch):
        lt = g * lax.dot_general(own_pnt, xn[b], (((1,), (1,)), ((), ())), preferred_element_type=F32)
        pos = lax.broadcasted_iota(jnp.int32, lt.shape, 1)
        lt = jnp.where(pos < len_ref[b], lt, NEG_FILL)
        d_exp = jnp.exp(lt - jnp.max(lt, axis=1, keepdims=True))
        z = jnp.sum(d_exp, axis=1, keepdims=True)
        slot_sum = jnp.dot(d_exp.astype(BF16), xg[b], preferred_element_type=F32)
        xs[b] = (slot_sum / z).astype(BF16)

    def y_rows(dev, e):
        return pl.ds(pl.multiple_of(dev * slots + e * per, per), per)

    def y_send(owner, e, rel, to, k, cols=None):
        block = yg.at[:, y_rows(owner, e), :] if cols is None else yg.at[:, y_rows(owner, e), cols]
        return pltpu.make_async_remote_copy(src_ref=block, dst_ref=block, send_sem=sy_sem.at[k],
                                            recv_sem=ry_sem.at[e, rel], device_id={"seq": to}, device_id_type=MESH)

    def send_own(e, cols=None):
        y_send(me, e, 1, xnb, 1, cols).start()
        y_send(me, e, 2, ynb, 2, cols).start()
        y_send(me, e, 3, dia, 3, cols).start()
        y_send(me, e, 0, part, 0, cols).start()

    def y_wait(e, rel):
        y_send(owners[rel], e, rel, part, 0).wait_recv()

    def forward(e):
        for rel in (1, 2, 3):
            y_wait(e, rel)
            y_send(owners[rel], e, rel + 3, part, rel + 3).start()

    fblk = 1024

    def hidden(e, slot):
        rows = xs[:, pl.ds(pl.multiple_of(e * per, per), per), :].reshape(batch * per, d_model)
        for f in range(ff // fblk):
            cols = pl.ds(f * fblk, fblk)
            up = jnp.dot(rows, w1b[slot, :, cols], preferred_element_type=F32)
            h_v[:, cols] = jax.nn.gelu(up).astype(BF16)

    def outputs(e, slot, c):
        cols = pl.ds(c * width, width)
        out = jnp.dot(h_v[...], w2b[slot, :, cols], preferred_element_type=F32).astype(BF16)
        yg[:, y_rows(me, e), cols] = out.reshape(batch, per, width)

    @pl.loop(0, n_exp - 1)
    def _(e):
        w1_copy(e).wait()
        hidden(e, e)
        w2_copy(e).wait()
        for c in range(chunks):
            outputs(e, e, c)
        send_own(e)

        @pl.when(e == 0)
        def _():
            w1_copy(n_exp - 1).start()
            for c in range(chunks):
                w2_last(c).start()

        @pl.when(e > 0)
        def _():
            forward(e - 1)

    last = n_exp - 1
    w1_copy(last).wait()
    hidden(last, last % ring)
    forward(last - 1)
    for c in range(chunks):
        w2_last(c).wait()
        outputs(last, last % ring, c)
        send_own(last, pl.ds(c * width, width))
    forward(last)
    for e in range(n_exp):
        for rel in (0, 4, 5, 6):
            y_wait(e, rel)

    first = me * tok
    for b in range(batch):
        mixed = jnp.dot(cw[b], yg[b], preferred_element_type=F32) / qs[b][:, :1]
        pos = first + lax.broadcasted_iota(jnp.int32, mixed.shape, 0)
        y_ref[b] = jnp.where(pos < len_ref[b], mixed, 0.0).astype(BF16)

    for copy in x_sends:
        copy.wait_send()
    for k in range(7):
        whole = yg.at[:, pl.ds(0, slots), :]
        pltpu.make_async_remote_copy(src_ref=whole, dst_ref=whole, send_sem=sy_sem.at[k], recv_sem=ry_sem.at[0, 0],
                                     device_id={"seq": part}, device_id_type=MESH).wait_send()


def solution(mesh):
    seq_size = mesh.shape["seq"]

    def local_layer(tok_blk, len_blk, slot_param, logit_scale, w_in, w_out):
        batch, tok, d_model = tok_blk.shape
        n_slots = slot_param.shape[1]
        n_exp, _, ff = w_in.shape
        slots = n_slots // seq_size
        ring = n_exp - 1
        chunks = 4
        dma = pltpu.SemaphoreType.DMA
        return pl.pallas_call(
            layer_kernel,
            out_shape=jax.ShapeDtypeStruct((batch, tok, d_model), BF16),
            in_specs=[pl.BlockSpec(memory_space=pltpu.SMEM)] * 2 + [pl.BlockSpec(memory_space=pltpu.HBM)] * 4,
            out_specs=pl.BlockSpec(memory_space=pltpu.VMEM),
            scratch_shapes=[
                pltpu.VMEM((batch, tok * seq_size, d_model), BF16),
                pltpu.VMEM((batch, tok * seq_size, d_model), BF16),
                pltpu.VMEM((d_model, n_slots), BF16),
                pltpu.VMEM((d_model, n_slots), BF16),
                pltpu.VMEM((2 * slots, d_model), BF16),
                pltpu.VMEM((batch, slots, d_model), BF16),
                pltpu.VMEM((batch * slots // n_exp, ff), BF16),
                pltpu.VMEM((batch, n_slots, d_model), BF16),
                pltpu.VMEM((batch, tok, n_slots), BF16),
                pltpu.VMEM((batch, tok, 128), F32),
                pltpu.VMEM((ring, d_model, ff), BF16),
                pltpu.VMEM((ring, ff, d_model), BF16),
                dma, dma, dma((ring,)), dma((ring,)), dma((chunks,)),
                dma((7,)), dma((7,)), dma((7,)), dma((n_exp, 7)),
            ],
            compiler_params=pltpu.CompilerParams(collective_id=0, has_side_effects=True, vmem_limit_bytes=60 * 1024 * 1024),
        )(len_blk, logit_scale.reshape(1, 1), tok_blk, slot_param, w_in, w_out)

    return jax.shard_map(local_layer, mesh=mesh, in_specs=(P("data", "seq", None), P("data"), P(None, None), P(), P("seq", None, None), P("seq", None, None)), out_specs=P("data", "seq", None), check_vma=False)
```

time: 164 us -> 50.8 us (0.31)
  waiting for transfers between devices: 81.1 us -> 0 us
  Pallas kernels: 0 us -> 48.5 us
  matrix products: 36.9 us -> 0 us
  blocking collectives: 25.1 us -> 0 us
  between operations: 13.8 us -> 0.66 us
  other arithmetic: 4.52 us -> 0 us
    pallas_call x0 -> x1, Pallas kernels: none -> 48.5 us  [local_layer(): pl.pallas_call(layer_kernel, out_shape=jax.ShapeDtypeStruct((batch, tok,...]
    dot_general x5 -> x0, matrix products: 36.9 us -> none  [the longest x1 16.6 us: local_layer(): jnp.einsum('besd,edf->besf', slot_grp, w_in, preferred_element_type=jnp.f...]
    reduce_scatter x1 -> x0, waiting for transfers between devices: 35 us -> none  [local_layer(): lax.psum_scatter(part_sum.astype(jnp.bfloat16), 'seq', scatter_dimension=...]
    pmax x1 -> x0, blocking collectives: 25.1 us -> none  [local_layer(): col_max = lax.pmax(jnp.max(masked, axis=1, keepdims=True), 'seq')]
    unnamed x4 -> x0, waiting for transfers between devices: 24.1 us -> none
    all_gather x1 -> x0, waiting for transfers between devices: 22.1 us -> none  [local_layer(): lax.all_gather(own_out.reshape(batch_loc, slot_loc, d_model), 'seq', axis...]
    reduce_sum x3 -> x0, other arithmetic: 2.7 us -> none  [the longest x2 2.52 us: l2_normed(): jnp.sum(v32 * v32, axis=axis_dim, keepdims=True) + EPSILON]
  transfers between devices with their start and end apart: 3 -> 0, of which waited for: 3 -> 0; matrix products, arithmetic and copies ran while one was open for 2% -> 0% of each run, Pallas kernels for 0% -> 0%
where the time goes in v1:
time: 50.8 us; the launch traced here: 50.7 us
  Pallas kernels  48.5 us (95%)
  local copies, waits for them, and re-layouts  1.57 us (3%)
  between operations  0.66 us (1%)
    pallas_call x1, Pallas kernels, local_layer(): pl.pallas_call(layer_kernel, out_shape=jax.ShapeDtypeStruct((batch, tok,...  48.5 us
    unnamed x1, local copies, waits for them, and re-layouts  1.57 us

profile of v1, /device:TPU:0, one launch (start us, length us, event | category | flops | bytes accessed | tf_op | source)
XLA Modules:
  0.0 50.7 jit_solution(10271298252736703824)
XLA Ops:
  0.7 48.5 %shard_map.64 = bf16[2,32,1024]{2,1,0:T(8,128)(2,1)} custom-call(s32[2]{0:T(128)} %len_ref.1, f32[1,1]{1,0:T(1,128)} %bitcast.1.g_ref, bf16[2,32,1024]{2,1,0:T(8,128)(2,1)} %x_hbm.1, bf16[1024,512]{1,0:T(8,128)(2,1)} %phi_hbm.1, bf16[4,1024,4096]{2,1,0:T(8,128)(2,1)} %w1_hbm.1, bf16[4,4096,1024]{2,1,0:T(8,128)(2,1)} %w2_hbm.1), custom_call_target="tpu_custom_call" | custom-call | tf_op jit(solution)/shard_map/pallas_call | solution.py:220
  49.2 1.6 %copy.9 = bf16[2,32,1024]{2,1,0:T(8,128)(2,1)} copy(bf16[2,32,1024]{2,1,0:T(8,128)(2,1)} %shard_map.64) | data formatting | bytes 262144

commit v2 on v1

--- a/solution.py
+++ b/solution.py
@@ -17,10 +17,10 @@
     return (v32 * lax.rsqrt(jnp.sum(v32 * v32, axis=-1, keepdims=True) + EPSILON)).astype(BF16)
 
 
-def layer_kernel(len_ref, g_ref, x_hbm, phi_hbm, w1_hbm, w2_hbm, y_ref,
-                 xg, xn, phi_v, pn, pnt, xs, h_v, yg, cw, qs, w1b, w2b,
-                 x_sem, phi_sem, w1_sem, w2_sem, w2l_sem,
-                 sx_sem, rx_sem, sy_sem, ry_sem):
+def layer_kernel(len_hbm, g_hbm, x_hbm, phi_hbm, w1_hbm, w2_hbm, y_ref,
+                 xg, xn, phi_v, pn, pnt, xs, h_v, yg, cw, qs, w1b, w2b, len_ref, g_ref,
+                 len_sem, g_sem, x_sem, phi_sem, w1_sem, w2_sem, w2l_sem,
+                 sx_sem, rx_sem, sy_sem, ry_sem, rl_sem):
     batch, tok, d_model = y_ref.shape
     n_exp = w1_hbm.shape[0]
     ff = w1_hbm.shape[2]
@@ -43,7 +43,7 @@
     owners = (part, xnb, ynb, dia, xnb + flip, ynb + flip, dia + flip)
 
     barrier = pltpu.get_barrier_semaphore()
-    for dev in owners[:4]:
+    for dev in owners[:3]:
         pl.semaphore_signal(barrier, inc=1, device_id={"seq": dev}, device_id_type=MESH)
 
     def tok_rows(dev):
@@ -53,6 +53,10 @@
     own_x.start()
     own_phi = pltpu.make_async_copy(phi_hbm, phi_v, phi_sem)
     own_phi.start()
+    own_len = pltpu.make_async_copy(len_hbm, len_ref, len_sem)
+    own_len.start()
+    own_g = pltpu.make_async_copy(g_hbm, g_ref, g_sem)
+    own_g.start()
 
     def w1_copy(e):
         return pltpu.make_async_copy(w1_hbm.at[e], w1b.at[lax.rem(e, ring)], w1_sem.at[lax.rem(e, ring)])
@@ -65,17 +69,18 @@
         return pltpu.make_async_copy(w2_hbm.at[n_exp - 1, :, cols], w2b.at[(n_exp - 1) % ring, :, cols], w2l_sem.at[c])
 
     for e in range(ring):
-        w1_copy(e).start()
-        w2_copy(e).start()
-
-    def x_send(owner, rel, to, k):
-        block = xg.at[:, tok_rows(owner), :]
-        return pltpu.make_async_remote_copy(src_ref=block, dst_ref=block, send_sem=sx_sem.at[k],
-                                            recv_sem=rx_sem.at[rel], device_id={"seq": to}, device_id_type=MESH)
+        w1_copy(e).start(priority=1)
+        w2_copy(e).start(priority=1)
+
+    def x_send(owner, half, rel, to, k):
+        block = xg.at[half, tok_rows(owner), :]
+        return pltpu.make_async_remote_copy(src_ref=block, dst_ref=block, send_sem=sx_sem.at[k, half],
+                                            recv_sem=rx_sem.at[rel, half], device_id={"seq": to}, device_id_type=MESH)
 
     own_x.wait()
-    pl.semaphore_wait(barrier, 4)
-    x_sends = [x_send(me, 1, xnb, 1), x_send(me, 2, ynb, 2), x_send(me, 3, dia, 3), x_send(me, 0, part, 0)]
+    pl.semaphore_wait(barrier, 3)
+    x_sends = [x_send(me, 0, 1, xnb, 1), x_send(me, 1, 2, ynb, 2), x_send(me, 1, 1, xnb, 1),
+               x_send(me, 0, 2, ynb, 2), x_send(me, 0, 0, part, 0), x_send(me, 1, 0, part, 0)]
     for copy in x_sends:
         copy.start()
 
@@ -86,33 +91,57 @@
         pn[:, cols] = (p32 * lax.rsqrt(jnp.sum(p32 * p32, axis=0, keepdims=True) + EPSILON)).astype(BF16)
     chip_cols = pl.ds(pl.multiple_of(chip * 128, 128), 128)
     pnt[...] = pn[:, chip_cols].T
-    g = g_ref[0, 0]
-
-    def normalise(dev):
-        for b in range(batch):
-            xn[b, tok_rows(dev), :] = row_normed(xg[b, tok_rows(dev), :])
-
-    normalise(me)
+    own_g.wait()
+    own_len.wait()
+    g = g_ref[0]
+
+    def normalise(dev, half):
+        xn[half, tok_rows(dev), :] = row_normed(xg[half, tok_rows(dev), :])
+
+    normalise(me, 0)
+    normalise(me, 1)
     for b in range(batch):
         own_l = g * jnp.dot(xn[b, tok_rows(me), :], pn[...], preferred_element_type=F32)
         c_exp = jnp.exp(own_l - jnp.max(own_l, axis=1, keepdims=True))
         cw[b] = c_exp.astype(BF16)
         qs[b] = jnp.broadcast_to(jnp.sum(c_exp, axis=1, keepdims=True), qs.shape[1:])
 
-    def x_wait(rel):
-        x_send(owners[rel], rel, part, 0).wait_recv()
-
-    x_wait(0)
-    normalise(owners[0])
-    for rel in (1, 2, 3):
-        x_wait(rel)
-        fwd = x_send(owners[rel], rel + 3, part, rel + 3)
-        fwd.start()
-        x_sends.append(fwd)
-        normalise(owners[rel])
-    for rel in (4, 5, 6):
-        x_wait(rel)
-        normalise(owners[rel])
+    def x_wait(rel, half):
+        x_send(owners[rel], half, rel, part, 0).wait_recv()
+
+    def x_pass(rel, half, to_rel, to, k):
+        copy = x_send(owners[rel], half, to_rel, to, k)
+        copy.start()
+        x_sends.append(copy)
+
+    x_wait(1, 0)
+    x_pass(1, 0, 3, ynb, 3)
+    x_pass(1, 0, 4, part, 4)
+    x_wait(2, 1)
+    x_pass(2, 1, 3, xnb, 3)
+    x_pass(2, 1, 5, part, 5)
+    normalise(owners[1], 0)
+    normalise(owners[2], 1)
+    for half in (0, 1):
+        x_wait(0, half)
+        normalise(owners[0], half)
+    x_wait(1, 1)
+    x_pass(1, 1, 4, part, 4)
+    x_wait(2, 0)
+    x_pass(2, 0, 5, part, 5)
+    normalise(owners[1], 1)
+    normalise(owners[2], 0)
+    for rel, half in ((4, 0), (5, 1), (4, 1), (5, 0)):
+        x_wait(rel, half)
+        normalise(owners[rel], half)
+    for half in (0, 1):
+        x_wait(3, half)
+        x_pass(3, half, 6, part, 6)
+    for half in (0, 1):
+        normalise(owners[3], half)
+    for half in (0, 1):
+        x_wait(6, half)
+        normalise(owners[6], half)
 
     own_pnt = pnt[pl.ds(pl.multiple_of(core * slots, slots), slots), :]
     for b in range(batch):
@@ -127,25 +156,37 @@
     def y_rows(dev, e):
         return pl.ds(pl.multiple_of(dev * slots + e * per, per), per)
 
-    def y_send(owner, e, rel, to, k, cols=None):
-        block = yg.at[:, y_rows(owner, e), :] if cols is None else yg.at[:, y_rows(owner, e), cols]
-        return pltpu.make_async_remote_copy(src_ref=block, dst_ref=block, send_sem=sy_sem.at[k],
-                                            recv_sem=ry_sem.at[e, rel], device_id={"seq": to}, device_id_type=MESH)
-
-    def send_own(e, cols=None):
-        y_send(me, e, 1, xnb, 1, cols).start()
-        y_send(me, e, 2, ynb, 2, cols).start()
-        y_send(me, e, 3, dia, 3, cols).start()
-        y_send(me, e, 0, part, 0, cols).start()
+    everything = slice(None)
+
+    def y_send(owner, e, to, send, recv, halves=everything, cols=everything):
+        block = yg.at[halves, y_rows(owner, e), cols]
+        return pltpu.make_async_remote_copy(src_ref=block, dst_ref=block, send_sem=send, recv_sem=recv,
+                                            device_id={"seq": to}, device_id_type=MESH)
+
+    def send_own(e):
+        y_send(me, e, xnb, sy_sem.at[1], ry_sem.at[e, 1]).start()
+        y_send(me, e, ynb, sy_sem.at[2], ry_sem.at[e, 2]).start()
+        y_send(me, e, part, sy_sem.at[0], ry_sem.at[e, 0]).start()
 
     def y_wait(e, rel):
-        y_send(owners[rel], e, rel, part, 0).wait_recv()
-
-    def forward(e):
-        for rel in (1, 2, 3):
-            y_wait(e, rel)
-            y_send(owners[rel], e, rel + 3, part, rel + 3).start()
-
+        y_send(owners[rel], e, part, sy_sem.at[0], ry_sem.at[e, rel]).wait_recv()
+
+    def near(e):
+        y_wait(e, 1)
+        y_send(owners[1], e, ynb, sy_sem.at[7], ry_sem.at[e, 3], halves=pl.ds(0, 1)).start()
+        y_send(owners[1], e, part, sy_sem.at[4], ry_sem.at[e, 4]).start()
+        y_wait(e, 2)
+        y_send(owners[2], e, xnb, sy_sem.at[8], ry_sem.at[e, 3], halves=pl.ds(1, 1)).start()
+        y_send(owners[2], e, part, sy_sem.at[5], ry_sem.at[e, 5]).start()
+
+    def far(e):
+        y_wait(e, 3)
+        y_send(owners[3], e, part, sy_sem.at[6], ry_sem.at[e, 6]).start()
+
+    def last_send(owner, c, rel, to, k):
+        return y_send(owner, last, to, sy_sem.at[k], rl_sem.at[c, rel], cols=pl.ds(c * width, width))
+
+    last = n_exp - 1
     fblk = 1024
 
     def hidden(e, slot):
@@ -171,26 +212,41 @@
 
         @pl.when(e == 0)
         def _():
-            w1_copy(n_exp - 1).start()
+            w1_copy(last).start(priority=1)
             for c in range(chunks):
-                w2_last(c).start()
+                w2_last(c).start(priority=1)
 
         @pl.when(e > 0)
         def _():
-            forward(e - 1)
-
-    last = n_exp - 1
+            near(e - 1)
+
+        @pl.when(e > 1)
+        def _():
+            far(e - 2)
+
     w1_copy(last).wait()
     hidden(last, last % ring)
-    forward(last - 1)
     for c in range(chunks):
         w2_last(c).wait()
         outputs(last, last % ring, c)
-        send_own(last, pl.ds(c * width, width))
-    forward(last)
-    for e in range(n_exp):
+        last_send(me, c, 1, xnb, 1).start()
+        last_send(me, c, 2, ynb, 2).start()
+        last_send(me, c, 3, dia, 3).start()
+        last_send(me, c, 0, part, 0).start()
+        if c == 0:
+            far(last - 2)
+            near(last - 1)
+    far(last - 1)
+    for c in range(chunks):
+        for rel in (1, 2, 3):
+            last_send(owners[rel], c, rel, part, 0).wait_recv()
+            last_send(owners[rel], c, rel + 3, part, rel + 3).start()
+    for e in range(last):
         for rel in (0, 4, 5, 6):
             y_wait(e, rel)
+    for c in range(chunks):
+        for rel in (0, 4, 5, 6):
+            last_send(owners[rel], c, rel, part, 0).wait_recv()
 
     first = me * tok
     for b in range(batch):
@@ -200,9 +256,14 @@
 
     for copy in x_sends:
         copy.wait_send()
-    for k in range(7):
-        whole = yg.at[:, pl.ds(0, slots), :]
-        pltpu.make_async_remote_copy(src_ref=whole, dst_ref=whole, send_sem=sy_sem.at[k], recv_sem=ry_sem.at[0, 0],
+    for k in range(9):
+        if k == 3:
+            sent = yg.at[:, pl.ds(0, per), :]
+        elif k > 6:
+            sent = yg.at[0, pl.ds(0, last * per), :]
+        else:
+            sent = yg.at[:, pl.ds(0, slots), :]
+        pltpu.make_async_remote_copy(src_ref=sent, dst_ref=sent, send_sem=sy_sem.at[k], recv_sem=ry_sem.at[0, 0],
                                      device_id={"seq": part}, device_id_type=MESH).wait_send()
 
 
@@ -220,7 +281,7 @@
         return pl.pallas_call(
             layer_kernel,
             out_shape=jax.ShapeDtypeStruct((batch, tok, d_model), BF16),
-            in_specs=[pl.BlockSpec(memory_space=pltpu.SMEM)] * 2 + [pl.BlockSpec(memory_space=pltpu.HBM)] * 4,
+            in_specs=[pl.BlockSpec(memory_space=pltpu.HBM)] * 6,
             out_specs=pl.BlockSpec(memory_space=pltpu.VMEM),
             scratch_shapes=[
                 pltpu.VMEM((batch, tok * seq_size, d_model), BF16),
@@ -235,10 +296,12 @@
                 pltpu.VMEM((batch, tok, 128), F32),
                 pltpu.VMEM((ring, d_model, ff), BF16),
                 pltpu.VMEM((ring, ff, d_model), BF16),
-                dma, dma, dma((ring,)), dma((ring,)), dma((chunks,)),
-                dma((7,)), dma((7,)), dma((7,)), dma((n_exp, 7)),
+                pltpu.SMEM((batch,), jnp.int32),
+                pltpu.SMEM((1,), F32),
+                dma, dma, dma, dma, dma((ring,)), dma((ring,)), dma((chunks,)),
+                dma((7, 2)), dma((7, 2)), dma((9,)), dma((n_exp, 7)), dma((chunks, 7)),
             ],
             compiler_params=pltpu.CompilerParams(collective_id=0, has_side_effects=True, vmem_limit_bytes=60 * 1024 * 1024),
-        )(len_blk, logit_scale.reshape(1, 1), tok_blk, slot_param, w_in, w_out)
+        )(len_blk, logit_scale.reshape(1), tok_blk, slot_param, w_in, w_out)
 
     return jax.shard_map(local_layer, mesh=mesh, in_specs=(P("data", "seq", None), P("data"), P(None, None), P(), P("seq", None, None), P("seq", None, None)), out_specs=P("data", "seq", None), check_vma=False)

time: 50.8 us -> 37.1 us (0.73)
  Pallas kernels: 48.5 us -> 34.8 us
    pallas_call x1, Pallas kernels: 48.5 us -> 34.8 us  [local_layer(): pl.pallas_call(layer_kernel, out_shape=jax.ShapeDtypeStruct((batch, tok,...]
where the time goes in v2:
time: 37.1 us; the launch traced here: 37 us
  Pallas kernels  34.8 us (94%)
  local copies, waits for them, and re-layouts  1.57 us (4%)
  between operations  0.66 us (2%)
    pallas_call x1, Pallas kernels, local_layer(): pl.pallas_call(layer_kernel, out_shape=jax.ShapeDtypeStruct((batch, tok,...  34.8 us
    unnamed x1, local copies, waits for them, and re-layouts  1.57 us

profile of v2, /device:TPU:0, one launch (start us, length us, event | category | flops | bytes accessed | tf_op | source)
XLA Modules:
  0.0 37.0 jit_solution(6586906179155315543)
XLA Ops:
  0.7 34.8 %shard_map.64 = bf16[2,32,1024]{2,1,0:T(8,128)(2,1)} custom-call(s32[2]{0:T(128)} %len_hbm.1, f32[1]{0:T(128)} %bitcast.1.g_hbm, bf16[2,32,1024]{2,1,0:T(8,128)(2,1)} %x_hbm.1, bf16[1024,512]{1,0:T(8,128)(2,1)} %phi_hbm.1, bf16[4,1024,4096]{2,1,0:T(8,128)(2,1)} %w1_hbm.1, bf16[4,4096,1024]{2,1,0:T(8,128)(2,1)} %w2_hbm.1), custom_call_target="tpu_custom_call" | custom-call | tf_op jit(solution)/shard_map/pallas_call | solution.py:281
  35.4 1.6 %copy.9 = bf16[2,32,1024]{2,1,0:T(8,128)(2,1)} copy(bf16[2,32,1024]{2,1,0:T(8,128)(2,1)} %shard_map.64) | data formatting | bytes 262144

commit v3 on v1

v3 whole, which is shorter than its diff:
```python
import functools

import jax
import jax.numpy as jnp
from jax import lax
from jax.experimental import pallas as pl
from jax.experimental.pallas import tpu as pltpu
from jax.sharding import PartitionSpec as P

EPSILON = 1e-6
NEG_FILL = -1e30
MESH = pl.DeviceIdType.MESH
F32 = jnp.float32
BF16 = jnp.bfloat16


def row_normed(v):
    v32 = v.astype(F32)
    return (v32 * lax.rsqrt(jnp.sum(v32 * v32, axis=-1, keepdims=True) + EPSILON)).astype(BF16)


def layer_kernel(sems, *refs):
    pl.run_scoped(lambda *scoped: layer_body(*refs, *scoped), *sems)


def layer_body(len_hbm, g_hbm, x_hbm, phi_hbm, w1_hbm, w2_hbm, y_ref,
                 xg, xn, phi_v, pn, pnt, xs, h_v, yg, cw, qs, w1b, w2b, len_ref, g_ref,
                 len_sem, g_sem, x_sem, phi_sem, w1_sem, w2_sem, w2l_sem,
                 sx_sem, rx_sem, sy_sem, ry_sem, rl_sem):
    batch, tok, d_model = y_ref.shape
    n_exp = w1_hbm.shape[0]
    ff = w1_hbm.shape[2]
    n_slots = phi_hbm.shape[1]
    all_tok = xg.shape[1]
    slots = xs.shape[1]
    per = slots // n_exp
    ring = w1b.shape[0]
    chunks = w2l_sem.shape[0]
    width = d_model // chunks
    last = n_exp - 1

    me = lax.axis_index("seq")
    core = lax.rem(me, 2)
    chip = lax.div(me, 2)
    part = me + 1 - 2 * core
    xsame = me + 2 - 4 * lax.rem(chip, 2)
    ysame = me + 4 - 8 * lax.div(chip, 2)
    dsame = xsame + ysame - me
    flip = 1 - 2 * core
    xnb, ynb, dia = xsame + flip, ysame + flip, dsame + flip
    owners = (part, xnb, ynb, dsame, xsame, ysame, dia)
    last_owners = (part, xnb, ynb, dia, xsame, ysame, dsame)

    barrier = pltpu.get_barrier_semaphore()
    for dev in owners[:3]:
        pl.semaphore_signal(barrier, inc=1, device_id={"seq": dev}, device_id_type=MESH)

    def tok_rows(dev):
        return pl.ds(pl.multiple_of(dev * tok, tok), tok)

    own_x = pltpu.make_async_copy(x_hbm, xg.at[:, tok_rows(me), :], x_sem)
    own_x.start()
    own_phi = pltpu.make_async_copy(phi_hbm, phi_v, phi_sem)
    own_phi.start()
    own_len = pltpu.make_async_copy(len_hbm, len_ref, len_sem)
    own_len.start()
    own_g = pltpu.make_async_copy(g_hbm, g_ref, g_sem)
    own_g.start()

    def w1_copy(e):
        return pltpu.make_async_copy(w1_hbm.at[e], w1b.at[lax.rem(e, ring)], w1_sem.at[lax.rem(e, ring)])

    def w2_copy(e):
        return pltpu.make_async_copy(w2_hbm.at[e], w2b.at[lax.rem(e, ring)], w2_sem.at[lax.rem(e, ring)])

    def w2_last(c):
        cols = pl.ds(c * width, width)
        return pltpu.make_async_copy(w2_hbm.at[n_exp - 1, :, cols], w2b.at[(n_exp - 1) % ring, :, cols], w2l_sem.at[c])

    for e in range(ring):
        w1_copy(e).start(priority=1)
        w2_copy(e).start(priority=1)

    quarter = tok // 2

    def x_block(owner, piece):
        return (piece // 2, pl.ds(pl.multiple_of(owner * tok + (piece % 2) * quarter, quarter), quarter))

    def x_send(owner, piece, rel, to, k):
        half, rows = x_block(owner, piece)
        block = xg.at[half, rows, :]
        return pltpu.make_async_remote_copy(src_ref=block, dst_ref=block, send_sem=sx_sem.at[k, piece],
                                            recv_sem=rx_sem.at[rel, piece], device_id={"seq": to}, device_id_type=MESH)

    own_x.wait()
    pl.semaphore_wait(barrier, 3)
    x_sends = []

    def x_start(owner, piece, rel, to, k):
        copy = x_send(owner, piece, rel, to, k)
        copy.start()
        x_sends.append(copy)

    for piece in range(4):
        x_start(me, piece, 1, xnb, 1)
        x_start(me, (piece + 2) % 4, 2, ynb, 2)
    for piece in range(4):
        x_start(me, piece, 0, part, 0)

    own_phi.wait()
    for c in range(n_slots // 128):
        cols = pl.ds(c * 128, 128)
        p32 = phi_v[:, cols].astype(F32)
        pn[:, cols] = (p32 * lax.rsqrt(jnp.sum(p32 * p32, axis=0, keepdims=True) + EPSILON)).astype(BF16)
    chip_cols = pl.ds(pl.multiple_of(chip * 128, 128), 128)
    pnt[...] = pn[:, chip_cols].T
    own_g.wait()
    own_len.wait()
    g = g_ref[0]

    def normalise(dev, piece):
        half, rows = x_block(dev, piece)
        xn[half, rows, :] = row_normed(xg[half, rows, :])

    for piece in range(4):
        normalise(me, piece)
    for b in range(batch):
        own_l = g * jnp.dot(xn[b, tok_rows(me), :], pn[...], preferred_element_type=F32)
        c_exp = jnp.exp(own_l - jnp.max(own_l, axis=1, keepdims=True))
        cw[b] = c_exp.astype(BF16)
        qs[b] = jnp.broadcast_to(jnp.sum(c_exp, axis=1, keepdims=True), qs.shape[1:])

    def x_wait(rel, piece):
        x_send(owners[rel], piece, rel, part, 0).wait_recv()

    for piece in (0, 1):
        x_wait(1, piece)
        x_start(owners[1], piece, 3, ynb, 3)
        x_start(owners[1], piece, 4, part, 4)
        x_wait(2, piece + 2)
        x_start(owners[2], piece + 2, 3, xnb, 3)
        x_start(owners[2], piece + 2, 5, part, 5)
    for piece in range(4):
        x_wait(0, piece)
        normalise(owners[0], piece)
    for piece in (0, 1):
        normalise(owners[1], piece)
        normalise(owners[2], piece + 2)
        x_wait(1, piece + 2)
        x_start(owners[1], piece + 2, 4, part, 4)
        x_wait(2, piece)
        x_start(owners[2], piece, 5, part, 5)
        normalise(owners[1], piece + 2)
        normalise(owners[2], piece)
    for piece in (0, 1):
        x_wait(4, piece)
        normalise(owners[4], piece)
        x_wait(5, piece + 2)
        normalise(owners[5], piece + 2)
    for piece in (0, 2, 1, 3):
        x_wait(3, piece)
        x_start(owners[3], piece, 6, part, 6)
        normalise(owners[3], piece)
    for piece in (0, 1):
        x_wait(4, piece + 2)
        normalise(owners[4], piece + 2)
        x_wait(5, piece)
        normalise(owners[5], piece)
    for piece in (0, 2, 1, 3):
        x_wait(6, piece)
        normalise(owners[6], piece)

    own_pnt = pnt[pl.ds(pl.multiple_of(core * slots, slots), slots), :]
    for b in range(batch):
        lt = g * lax.dot_general(own_pnt, xn[b], (((1,), (1,)), ((), ())), preferred_element_type=F32)
        pos = lax.broadcasted_iota(jnp.int32, lt.shape, 1)
        lt = jnp.where(pos < len_ref[b], lt, NEG_FILL)
        d_exp = jnp.exp(lt - jnp.max(lt, axis=1, keepdims=True))
        z = jnp.sum(d_exp, axis=1, keepdims=True)
        slot_sum = jnp.dot(d_exp.astype(BF16), xg[b], preferred_element_type=F32)
        xs[b] = (slot_sum / z).astype(BF16)

    def y_rows(dev, e):
        return pl.ds(pl.multiple_of(dev * slots + e * per, per), per)

    def y_send(owner, e, rel, to, recv, cols=slice(None)):
        block = yg.at[:, y_rows(owner, e), cols]
        return pltpu.make_async_remote_copy(src_ref=block, dst_ref=block, send_sem=sy_sem.at[rel], recv_sem=recv,
                                            device_id={"seq": to}, device_id_type=MESH)

    def y_chunk(owner, e, c, rel, to, recv):
        return y_send(owner, e, rel, to, recv, pl.ds(c * width, width))

    def send_own(e, cols, recvs):
        for rel, to in ((3, dia), (1, xnb), (2, ynb), (0, part)):
            y_send(me, e, rel, to, recvs.at[rel], cols).start()

    def y_wait(e, rel):
        y_send(last_owners[rel], e, rel, part, ry_sem.at[e, rel]).wait_recv()

    def forward(e):
        for rel in (1, 2, 3):
            y_wait(e, rel)
            y_send(last_owners[rel], e, rel + 3, part, ry_sem.at[e, rel + 3]).start()

    fblk = 1024

    def hidden(e, slot):
        rows = xs[:, pl.ds(pl.multiple_of(e * per, per), per), :].reshape(batch * per, d_model)
        for f in range(ff // fblk):
            cols = pl.ds(f * fblk, fblk)
            up = jnp.dot(rows, w1b[slot, :, cols], preferred_element_type=F32)
            h_v[:, cols] = jax.nn.gelu(up).astype(BF16)

    def outputs(e, slot, cols):
        out = jnp.dot(h_v[...], w2b[slot, :, cols], preferred_element_type=F32).astype(BF16)
        yg[:, y_rows(me, e), cols] = out.reshape(batch, per, cols.size)

    @pl.loop(0, n_exp - 1)
    def _(e):
        w1_copy(e).wait()
        hidden(e, e)

        @pl.when(e == 0)
        def _():
            w1_copy(last).start(priority=1)

        w2_copy(e).wait()
        for c in range(2):
            outputs(e, e, pl.ds(c * 2 * width, 2 * width))
            send_own(e, pl.ds(c * 2 * width, 2 * width), ry_sem.at[e])

        @pl.when(e == 0)
        def _():
            for c in range(chunks):
                w2_last(c).start(priority=1)

        @pl.when(e > 0)
        def _():
            forward(e - 1)

    w1_copy(last).wait()
    hidden(last, last % ring)
    for c in range(chunks):
        w2_last(c).wait()
        outputs(last, last % ring, pl.ds(c * width, width))
        send_own(last, pl.ds(c * width, width), rl_sem.at[c])
    forward(last - 1)
    for c in range(chunks):
        for rel in (1, 2, 3):
            y_chunk(last_owners[rel], last, c, rel, part, rl_sem.at[c, rel]).wait_recv()
            y_chunk(last_owners[rel], last, c, rel + 3, part, rl_sem.at[c, rel + 3]).start()
    for e in range(last):
        for rel in (0, 4, 5, 6):
            y_wait(e, rel)
    for c in range(chunks):
        for rel in (0, 4, 5, 6):
            y_chunk(last_owners[rel], last, c, rel, part, rl_sem.at[c, rel]).wait_recv()

    first = me * tok
    for b in range(batch):
        mixed = jnp.dot(cw[b], yg[b], preferred_element_type=F32) / qs[b][:, :1]
        pos = first + lax.broadcasted_iota(jnp.int32, mixed.shape, 0)
        y_ref[b] = jnp.where(pos < len_ref[b], mixed, 0.0).astype(BF16)

    for copy in x_sends:
        copy.wait_send()
    for rel in range(7):
        sent = yg.at[:, pl.ds(0, slots), :]
        pltpu.make_async_remote_copy(src_ref=sent, dst_ref=sent, send_sem=sy_sem.at[rel], recv_sem=ry_sem.at[0, rel],
                                     device_id={"seq": part}, device_id_type=MESH).wait_send()


def solution(mesh):
    seq_size = mesh.shape["seq"]

    def local_layer(tok_blk, len_blk, slot_param, logit_scale, w_in, w_out):
        batch, tok, d_model = tok_blk.shape
        n_slots = slot_param.shape[1]
        n_exp, _, ff = w_in.shape
        slots = n_slots // seq_size
        ring = n_exp - 1
        chunks = 4
        dma = pltpu.SemaphoreType.DMA
        sems = (dma, dma, dma, dma, dma((ring,)), dma((ring,)), dma((chunks,)),
                dma((7, 4)), dma((7, 4)), dma((7,)), dma((n_exp, 7)), dma((chunks, 7)))
        return pl.pallas_call(
            functools.partial(layer_kernel, sems),
            out_shape=pltpu.VMEM((batch, tok, d_model), BF16),
            in_specs=[pl.BlockSpec(memory_space=pltpu.HBM)] * 6,
            out_specs=pl.BlockSpec(memory_space=pltpu.VMEM),
            scratch_shapes=[
                pltpu.VMEM((batch, tok * seq_size, d_model), BF16),
                pltpu.VMEM((batch, tok * seq_size, d_model), BF16),
                pltpu.VMEM((d_model, n_slots), BF16),
                pltpu.VMEM((d_model, n_slots), BF16),
                pltpu.VMEM((2 * slots, d_model), BF16),
                pltpu.VMEM((batch, slots, d_model), BF16),
                pltpu.VMEM((batch * slots // n_exp, ff), BF16),
                pltpu.VMEM((batch, n_slots, d_model), BF16),
                pltpu.VMEM((batch, tok, n_slots), BF16),
                pltpu.VMEM((batch, tok, 128), F32),
                pltpu.VMEM((ring, d_model, ff), BF16),
                pltpu.VMEM((ring, ff, d_model), BF16),
                pltpu.SMEM((batch,), jnp.int32),
                pltpu.SMEM((1,), F32),
            ],
            compiler_params=pltpu.CompilerParams(collective_id=0, has_side_effects=True, vmem_limit_bytes=60 * 1024 * 1024),
        )(len_blk, logit_scale.reshape(1), tok_blk, slot_param, w_in, w_out)

    return jax.shard_map(local_layer, mesh=mesh, in_specs=(P("data", "seq", None), P("data"), P(None, None), P(), P("seq", None, None), P("seq", None, None)), out_specs=P("data", "seq", None), check_vma=False)
```

time: 50.8 us -> 32.9 us (0.65)
  Pallas kernels: 48.5 us -> 31.5 us
  local copies, waits for them, and re-layouts: 1.57 us -> 0.66 us
    pallas_call x1, Pallas kernels: 48.5 us -> 31.5 us  [local_layer(): pl.pallas_call(functools.partial(layer_kernel, sems), out_shape=pltpu.VME...]
    unnamed x1, local copies, waits for them, and re-layouts: 1.57 us -> 0.66 us
where the time goes in v3:
time: 32.9 us; the launch traced here: 32.8 us
  Pallas kernels  31.5 us (96%)
  local copies, waits for them, and re-layouts  0.66 us (2%)
  between operations  0.66 us (2%)
    pallas_call x1, Pallas kernels, local_layer(): pl.pallas_call(functools.partial(layer_kernel, sems), out_shape=pltpu.VME...  31.5 us

profile of v3, /device:TPU:0, one launch (start us, length us, event | category | flops | bytes accessed | tf_op | source)
XLA Modules:
  0.0 32.8 jit_solution(4567167904734720817)
XLA Ops:
  0.7 31.5 %shard_map.64 = bf16[2,32,1024]{2,1,0:T(8,128)(2,1)S(1)} custom-call(s32[2]{0:T(128)} %refs_0_.1, f32[1]{0:T(128)} %bitcast.1.refs_1_, bf16[2,32,1024]{2,1,0:T(8,128)(2,1)} %refs_2_.1, bf16[1024,512]{1,0:T(8,128)(2,1)} %refs_3_.1, bf16[4,1024,4096]{2,1,0:T(8,128)(2,1)} %refs_4_.1, bf16[4,4096,1024]{2,1,0:T(8,128)(2,1)} %refs_5_.1), custom_call_target="tpu_custom_call" | custom-call | tf_op jit(solution)/shard_map/pallas_call | solution.py:287
  32.1 0.7 %copy.8 = bf16[2,32,1024]{2,1,0:T(8,128)(2,1)} copy(bf16[2,32,1024]{2,1,0:T(8,128)(2,1)S(1)} %shard_map.64) | data formatting | bytes 262144

commit v4 on v3

--- a/solution.py
+++ b/solution.py
@@ -24,14 +24,13 @@
 
 
 def layer_body(len_hbm, g_hbm, x_hbm, phi_hbm, w1_hbm, w2_hbm, y_ref,
-                 xg, xn, phi_v, pn, pnt, xs, h_v, yg, cw, qs, w1b, w2b, len_ref, g_ref,
+                 xg, xn, la, phi_v, pn, pnt, xs, h_v, yg, cw, qs, w1b, w2b, len_ref, g_ref,
                  len_sem, g_sem, x_sem, phi_sem, w1_sem, w2_sem, w2l_sem,
                  sx_sem, rx_sem, sy_sem, ry_sem, rl_sem):
     batch, tok, d_model = y_ref.shape
     n_exp = w1_hbm.shape[0]
     ff = w1_hbm.shape[2]
     n_slots = phi_hbm.shape[1]
-    all_tok = xg.shape[1]
     slots = xs.shape[1]
     per = slots // n_exp
     ring = w1b.shape[0]
@@ -55,11 +54,18 @@
     for dev in owners[:3]:
         pl.semaphore_signal(barrier, inc=1, device_id={"seq": dev}, device_id_type=MESH)
 
-    def tok_rows(dev):
-        return pl.ds(pl.multiple_of(dev * tok, tok), tok)
-
-    own_x = pltpu.make_async_copy(x_hbm, xg.at[:, tok_rows(me), :], x_sem)
-    own_x.start()
+    quarter = tok // 2
+    slot_of = (1, 2, 3, 6, 4, 5, 7)
+
+    def x_block(slot, piece):
+        return xg.at[piece // 2, slot, pl.ds((piece % 2) * quarter, quarter), :]
+
+    def own_x(piece):
+        rows = pl.ds((piece % 2) * quarter, quarter)
+        return pltpu.make_async_copy(x_hbm.at[piece // 2, rows, :], x_block(0, piece), x_sem.at[piece])
+
+    for piece in (0, 2, 1, 3):
+        own_x(piece).start()
     own_phi = pltpu.make_async_copy(phi_hbm, phi_v, phi_sem)
     own_phi.start()
     own_len = pltpu.make_async_copy(len_hbm, len_ref, len_sem)
@@ -81,31 +87,32 @@
         w1_copy(e).start(priority=1)
         w2_copy(e).start(priority=1)
 
-    quarter = tok // 2
-
-    def x_block(owner, piece):
-        return (piece // 2, pl.ds(pl.multiple_of(owner * tok + (piece % 2) * quarter, quarter), quarter))
-
-    def x_send(owner, piece, rel, to, k):
-        half, rows = x_block(owner, piece)
-        block = xg.at[half, rows, :]
-        return pltpu.make_async_remote_copy(src_ref=block, dst_ref=block, send_sem=sx_sem.at[k, piece],
-                                            recv_sem=rx_sem.at[rel, piece], device_id={"seq": to}, device_id_type=MESH)
-
-    own_x.wait()
-    pl.semaphore_wait(barrier, 3)
+    def x_send(slot, piece, rel, to, k):
+        return pltpu.make_async_remote_copy(src_ref=x_block(slot, piece), dst_ref=x_block(slot_of[rel], piece),
+                                            send_sem=sx_sem.at[k, piece], recv_sem=rx_sem.at[rel, piece],
+                                            device_id={"seq": to}, device_id_type=MESH)
+
     x_sends = []
 
-    def x_start(owner, piece, rel, to, k):
-        copy = x_send(owner, piece, rel, to, k)
+    def x_start(slot, piece, rel, to, k):
+        copy = x_send(slot, piece, rel, to, k)
         copy.start()
         x_sends.append(copy)
 
+    pl.semaphore_wait(barrier, 3)
+    own_x(0).wait()
+    x_start(0, 0, 1, xnb, 1)
+    own_x(2).wait()
+    x_start(0, 2, 2, ynb, 2)
+    own_x(1).wait()
+    x_start(0, 1, 1, xnb, 1)
+    own_x(3).wait()
+    x_start(0, 3, 2, ynb, 2)
+    for piece in (0, 1):
+        x_start(0, piece + 2, 1, xnb, 1)
+        x_start(0, piece, 2, ynb, 2)
     for piece in range(4):
-        x_start(me, piece, 1, xnb, 1)
-        x_start(me, (piece + 2) % 4, 2, ynb, 2)
-    for piece in range(4):
-        x_start(me, piece, 0, part, 0)
+        x_start(0, piece, 0, part, 0)
 
     own_phi.wait()
     for c in range(n_slots // 128):
@@ -118,67 +125,71 @@
     own_len.wait()
     g = g_ref[0]
 
-    def normalise(dev, piece):
-        half, rows = x_block(dev, piece)
-        xn[half, rows, :] = row_normed(xg[half, rows, :])
-
-    for piece in range(4):
-        normalise(me, piece)
+    def normalise(slot):
+        for b in range(batch):
+            xn[b, slot] = row_normed(xg[b, slot])
+
+    normalise(0)
     for b in range(batch):
-        own_l = g * jnp.dot(xn[b, tok_rows(me), :], pn[...], preferred_element_type=F32)
+        own_l = g * jnp.dot(xn[b, 0], pn[...], preferred_element_type=F32)
         c_exp = jnp.exp(own_l - jnp.max(own_l, axis=1, keepdims=True))
         cw[b] = c_exp.astype(BF16)
         qs[b] = jnp.broadcast_to(jnp.sum(c_exp, axis=1, keepdims=True), qs.shape[1:])
 
+    own_pnt = pnt[pl.ds(pl.multiple_of(core * slots, slots), slots), :]
+    near_tok = 4 * tok
+
+    def slot_logits(b, half):
+        rows = xn[b, 4 * half:4 * half + 4].reshape(near_tok, d_model)
+        lt = g * lax.dot_general(own_pnt, rows, (((1,), (1,)), ((), ())), preferred_element_type=F32)
+        lane = lax.broadcasted_iota(jnp.int32, lt.shape, 1)
+        pos = lane
+        for n, slot in enumerate(range(4 * half, 4 * half + 4)):
+            owner = me if slot == 0 else owners[slot_of.index(slot)]
+            pos = jnp.where(lane >= n * tok, lane + (owner - n) * tok, pos)
+        return jnp.where(pos < len_ref[b], lt, NEG_FILL)
+
     def x_wait(rel, piece):
-        x_send(owners[rel], piece, rel, part, 0).wait_recv()
+        x_send(0, piece, rel, part, 0).wait_recv()
 
     for piece in (0, 1):
         x_wait(1, piece)
-        x_start(owners[1], piece, 3, ynb, 3)
-        x_start(owners[1], piece, 4, part, 4)
+        x_start(2, piece, 3, ynb, 3)
+        x_start(2, piece, 4, part, 4)
         x_wait(2, piece + 2)
-        x_start(owners[2], piece + 2, 3, xnb, 3)
-        x_start(owners[2], piece + 2, 5, part, 5)
+        x_start(3, piece + 2, 3, xnb, 3)
+        x_start(3, piece + 2, 5, part, 5)
     for piece in range(4):
         x_wait(0, piece)
-        normalise(owners[0], piece)
+    normalise(1)
     for piece in (0, 1):
-        normalise(owners[1], piece)
-        normalise(owners[2], piece + 2)
         x_wait(1, piece + 2)
-        x_start(owners[1], piece + 2, 4, part, 4)
+        x_start(2, piece + 2, 4, part, 4)
         x_wait(2, piece)
-        x_start(owners[2], piece, 5, part, 5)
-        normalise(owners[1], piece + 2)
-        normalise(owners[2], piece)
-    for piece in (0, 1):
-        x_wait(4, piece)
-        normalise(owners[4], piece)
-        x_wait(5, piece + 2)
-        normalise(owners[5], piece + 2)
+        x_start(3, piece, 5, part, 5)
+    normalise(2)
+    normalise(3)
+    for b in range(batch):
+        la[b] = slot_logits(b, 0)
     for piece in (0, 2, 1, 3):
         x_wait(3, piece)
-        x_start(owners[3], piece, 6, part, 6)
-        normalise(owners[3], piece)
-    for piece in (0, 1):
-        x_wait(4, piece + 2)
-        normalise(owners[4], piece + 2)
-        x_wait(5, piece)
-        normalise(owners[5], piece)
-    for piece in (0, 2, 1, 3):
+        x_start(6, piece, 6, part, 6)
+    for rel in (4, 5):
+        for piece in range(4):
+            x_wait(rel, piece)
+    for slot in (4, 5, 6):
+        normalise(slot)
+    for piece in range(4):
         x_wait(6, piece)
-        normalise(owners[6], piece)
-
-    own_pnt = pnt[pl.ds(pl.multiple_of(core * slots, slots), slots), :]
+    normalise(7)
     for b in range(batch):
-        lt = g * lax.dot_general(own_pnt, xn[b], (((1,), (1,)), ((), ())), preferred_element_type=F32)
-        pos = lax.broadcasted_iota(jnp.int32, lt.shape, 1)
-        lt = jnp.where(pos < len_ref[b], lt, NEG_FILL)
-        d_exp = jnp.exp(lt - jnp.max(lt, axis=1, keepdims=True))
+        near, far = la[b], slot_logits(b, 1)
+        top = jnp.maximum(jnp.max(near, axis=1, keepdims=True), jnp.max(far, axis=1, keepdims=True))
+        d_exp = jnp.concatenate([jnp.exp(near - top), jnp.exp(far - top)], axis=1)
         z = jnp.sum(d_exp, axis=1, keepdims=True)
-        slot_sum = jnp.dot(d_exp.astype(BF16), xg[b], preferred_element_type=F32)
-        xs[b] = (slot_sum / z).astype(BF16)
+        tokens = xg[b].reshape(2 * near_tok, d_model)
+        slot_sum = jnp.dot(d_exp.astype(BF16), tokens, preferred_element_type=F32)
+        xs[b] = (slot_sum / z).astype(BF16).astype(F32)
 
     def y_rows(dev, e):
         return pl.ds(pl.multiple_of(dev * slots + e * per, per), per)
@@ -210,7 +221,7 @@
         for f in range(ff // fblk):
             cols = pl.ds(f * fblk, fblk)
             up = jnp.dot(rows, w1b[slot, :, cols], preferred_element_type=F32)
-            h_v[:, cols] = jax.nn.gelu(up).astype(BF16)
+            h_v[:, cols] = jax.nn.gelu(up).astype(BF16).astype(F32)
 
     def outputs(e, slot, cols):
         out = jnp.dot(h_v[...], w2b[slot, :, cols], preferred_element_type=F32).astype(BF16)
@@ -219,13 +230,13 @@
     @pl.loop(0, n_exp - 1)
     def _(e):
         w1_copy(e).wait()
+        w2_copy(e).wait()
         hidden(e, e)
 
         @pl.when(e == 0)
         def _():
             w1_copy(last).start(priority=1)
 
-        w2_copy(e).wait()
         for c in range(2):
             outputs(e, e, pl.ds(c * 2 * width, 2 * width))
             send_own(e, pl.ds(c * 2 * width, 2 * width), ry_sem.at[e])
@@ -235,9 +246,9 @@
             for c in range(chunks):
                 w2_last(c).start(priority=1)
 
-        @pl.when(e > 0)
+        @pl.when(e > 1)
         def _():
-            forward(e - 1)
+            forward(e - 2)
 
     w1_copy(last).wait()
     hidden(last, last % ring)
@@ -245,6 +256,8 @@
         w2_last(c).wait()
         outputs(last, last % ring, pl.ds(c * width, width))
         send_own(last, pl.ds(c * width, width), rl_sem.at[c])
+        if c == 0:
+            forward(last - 2)
     forward(last - 1)
     for c in range(chunks):
         for rel in (1, 2, 3):
@@ -282,7 +295,7 @@
         ring = n_exp - 1
         chunks = 4
         dma = pltpu.SemaphoreType.DMA
-        sems = (dma, dma, dma, dma, dma((ring,)), dma((ring,)), dma((chunks,)),
+        sems = (dma, dma, dma((4,)), dma, dma((ring,)), dma((ring,)), dma((chunks,)),
                 dma((7, 4)), dma((7, 4)), dma((7,)), dma((n_exp, 7)), dma((chunks, 7)))
         return pl.pallas_call(
             functools.partial(layer_kernel, sems),
@@ -290,13 +303,14 @@
             in_specs=[pl.BlockSpec(memory_space=pltpu.HBM)] * 6,
             out_specs=pl.BlockSpec(memory_space=pltpu.VMEM),
             scratch_shapes=[
-                pltpu.VMEM((batch, tok * seq_size, d_model), BF16),
-                pltpu.VMEM((batch, tok * seq_size, d_model), BF16),
+                pltpu.VMEM((batch, seq_size, tok, d_model), BF16),
+                pltpu.VMEM((batch, seq_size, tok, d_model), BF16),
+                pltpu.VMEM((batch, slots, tok * seq_size // 2), F32),
                 pltpu.VMEM((d_model, n_slots), BF16),
                 pltpu.VMEM((d_model, n_slots), BF16),
                 pltpu.VMEM((2 * slots, d_model), BF16),
-                pltpu.VMEM((batch, slots, d_model), BF16),
-                pltpu.VMEM((batch * slots // n_exp, ff), BF16),
+                pltpu.VMEM((batch, slots, d_model), F32),
+                pltpu.VMEM((batch * slots // n_exp, ff), F32),
                 pltpu.VMEM((batch, n_slots, d_model), BF16),
                 pltpu.VMEM((batch, tok, n_slots), BF16),
                 pltpu.VMEM((batch, tok, 128), F32),

time: 32.9 us -> 31.3 us (0.951)
  Pallas kernels: 31.5 us -> 29.9 us
    pallas_call x1, Pallas kernels: 31.5 us -> 29.9 us  [local_layer(): pl.pallas_call(functools.partial(layer_kernel, sems), out_shape=pltpu.VME...]
where the time goes in v4:
time: 31.3 us; the launch traced here: 31.2 us
  Pallas kernels  29.9 us (96%)
  local copies, waits for them, and re-layouts  0.66 us (2%)
  between operations  0.66 us (2%)
    pallas_call x1, Pallas kernels, local_layer(): pl.pallas_call(functools.partial(layer_kernel, sems), out_shape=pltpu.VME...  29.9 us
    unnamed x1, local copies, waits for them, and re-layouts  0.66 us

profile of v4, /device:TPU:0, one launch (start us, length us, event | category | flops | bytes accessed | tf_op | source)
XLA Modules:
  0.0 31.2 jit_solution(14536110348621402458)
XLA Ops:
  0.7 29.9 %shard_map.64 = bf16[2,32,1024]{2,1,0:T(8,128)(2,1)S(1)} custom-call(s32[2]{0:T(128)} %refs_0_.1, f32[1]{0:T(128)} %bitcast.1.refs_1_, bf16[2,32,1024]{2,1,0:T(8,128)(2,1)} %refs_2_.1, bf16[1024,512]{1,0:T(8,128)(2,1)} %refs_3_.1, bf16[4,1024,4096]{2,1,0:T(8,128)(2,1)} %refs_4_.1, bf16[4,4096,1024]{2,1,0:T(8,128)(2,1)} %refs_5_.1), custom_call_target="tpu_custom_call" | custom-call | tf_op jit(solution)/shard_map/pallas_call | solution.py:300
  30.6 0.7 %copy.8 = bf16[2,32,1024]{2,1,0:T(8,128)(2,1)} copy(bf16[2,32,1024]{2,1,0:T(8,128)(2,1)S(1)} %shard_map.64) | data formatting | bytes 262144

commit v5 on v4

--- a/solution.py
+++ b/solution.py
@@ -58,11 +58,11 @@
     slot_of = (1, 2, 3, 6, 4, 5, 7)
 
     def x_block(slot, piece):
-        return xg.at[piece // 2, slot, pl.ds((piece % 2) * quarter, quarter), :]
+        return xg.at[piece % 2, slot, pl.ds((piece // 2) * quarter, quarter), :]
 
     def own_x(piece):
-        rows = pl.ds((piece % 2) * quarter, quarter)
-        return pltpu.make_async_copy(x_hbm.at[piece // 2, rows, :], x_block(0, piece), x_sem.at[piece])
+        rows = pl.ds((piece // 2) * quarter, quarter)
+        return pltpu.make_async_copy(x_hbm.at[piece % 2, rows, :], x_block(0, piece), x_sem.at[piece])
 
     for piece in (0, 2, 1, 3):
         own_x(piece).start()
@@ -179,10 +179,10 @@
             x_wait(rel, piece)
     for slot in (4, 5, 6):
         normalise(slot)
-    for piece in range(4):
-        x_wait(6, piece)
-    normalise(7)
     for b in range(batch):
+        x_wait(6, b)
+        x_wait(6, b + 2)
+        xn[b, 7] = row_normed(xg[b, 7])
         near, far = la[b], slot_logits(b, 1)
         top = jnp.maximum(jnp.max(near, axis=1, keepdims=True), jnp.max(far, axis=1, keepdims=True))
         d_exp = jnp.concatenate([jnp.exp(near - top), jnp.exp(far - top)], axis=1)
@@ -216,26 +216,34 @@
 
     fblk = 1024
 
-    def hidden(e, slot):
+    def hidden(e, slot, negate_high=False):
         rows = xs[:, pl.ds(pl.multiple_of(e * per, per), per), :].reshape(batch * per, d_model)
         for f in range(ff // fblk):
             cols = pl.ds(f * fblk, fblk)
             up = jnp.dot(rows, w1b[slot, :, cols], preferred_element_type=F32)
-            h_v[:, cols] = jax.nn.gelu(up).astype(BF16).astype(F32)
+            act = jax.nn.gelu(up).astype(BF16).astype(F32)
+            h_v[:, cols] = -act if negate_high and f * fblk >= ff // 2 else act
 
     def outputs(e, slot, cols):
-        out = jnp.dot(h_v[...], w2b[slot, :, cols], preferred_element_type=F32).astype(BF16)
+        if cols.size > width:
+            out = jnp.dot(h_v[...], w2b[slot, :, cols], preferred_element_type=F32)
+        else:
+            low, high = pl.ds(0, ff // 2), pl.ds(ff // 2, ff // 2)
+            out = (jnp.dot(h_v[:, low], w2b[slot, low, cols], preferred_element_type=F32)
+                   - jnp.dot(h_v[:, high], w2b[slot, high, cols], preferred_element_type=F32))
+        out = out.astype(BF16)
         yg[:, y_rows(me, e), cols] = out.reshape(batch, per, cols.size)
 
     @pl.loop(0, n_exp - 1)
     def _(e):
         w1_copy(e).wait()
-        w2_copy(e).wait()
         hidden(e, e)
 
         @pl.when(e == 0)
         def _():
             w1_copy(last).start(priority=1)
+
+        w2_copy(e).wait()
 
         for c in range(2):
             outputs(e, e, pl.ds(c * 2 * width, 2 * width))
@@ -251,7 +259,7 @@
             forward(e - 2)
 
     w1_copy(last).wait()
-    hidden(last, last % ring)
+    hidden(last, last % ring, True)
     for c in range(chunks):
         w2_last(c).wait()
         outputs(last, last % ring, pl.ds(c * width, width))
@@ -266,15 +274,15 @@
     for e in range(last):
         for rel in (0, 4, 5, 6):
             y_wait(e, rel)
+    first = me * tok
     for c in range(chunks):
         for rel in (0, 4, 5, 6):
             y_chunk(last_owners[rel], last, c, rel, part, rl_sem.at[c, rel]).wait_recv()
-
-    first = me * tok
-    for b in range(batch):
-        mixed = jnp.dot(cw[b], yg[b], preferred_element_type=F32) / qs[b][:, :1]
-        pos = first + lax.broadcasted_iota(jnp.int32, mixed.shape, 0)
-        y_ref[b] = jnp.where(pos < len_ref[b], mixed, 0.0).astype(BF16)
+        cols = pl.ds(c * width, width)
+        for b in range(batch):
+            mixed = jnp.dot(cw[b], yg[b, :, cols], preferred_element_type=F32) / qs[b][:, :1]
+            pos = first + lax.broadcasted_iota(jnp.int32, mixed.shape, 0)
+            y_ref[b, :, cols] = jnp.where(pos < len_ref[b], mixed, 0.0).astype(BF16)
 
     for copy in x_sends:
         copy.wait_send()

time: 31.3 us -> 30.5 us (0.974)
  Pallas kernels: 29.9 us -> 29.1 us
    pallas_call x1, Pallas kernels: 29.9 us -> 29.1 us  [local_layer(): pl.pallas_call(functools.partial(layer_kernel, sems), out_shape=pltpu.VME...]
where the time goes in v5:
time: 30.5 us; the launch traced here: 30.4 us
  Pallas kernels  29.1 us (95%)
  local copies, waits for them, and re-layouts  0.66 us (2%)
  between operations  0.66 us (2%)
    pallas_call x1, Pallas kernels, local_layer(): pl.pallas_call(functools.partial(layer_kernel, sems), out_shape=pltpu.VME...  29.1 us
    unnamed x1, local copies, waits for them, and re-layouts  0.66 us

profile of v5, /device:TPU:0, one launch (start us, length us, event | category | flops | bytes accessed | tf_op | source)
XLA Modules:
  0.0 30.4 jit_solution(3980084213180478090)
XLA Ops:
  0.7 29.1 %shard_map.64 = bf16[2,32,1024]{2,1,0:T(8,128)(2,1)S(1)} custom-call(s32[2]{0:T(128)} %refs_0_.1, f32[1]{0:T(128)} %bitcast.1.refs_1_, bf16[2,32,1024]{2,1,0:T(8,128)(2,1)} %refs_2_.1, bf16[1024,512]{1,0:T(8,128)(2,1)} %refs_3_.1, bf16[4,1024,4096]{2,1,0:T(8,128)(2,1)} %refs_4_.1, bf16[4,4096,1024]{2,1,0:T(8,128)(2,1)} %refs_5_.1), custom_call_target="tpu_custom_call" | custom-call | tf_op jit(solution)/shard_map/pallas_call | solution.py:308
  29.8 0.7 %copy.8 = bf16[2,32,1024]{2,1,0:T(8,128)(2,1)} copy(bf16[2,32,1024]{2,1,0:T(8,128)(2,1)S(1)} %shard_map.64) | data formatting | bytes 262144

commit v6 on v5

--- a/solution.py
+++ b/solution.py
@@ -25,7 +25,7 @@
 
 def layer_body(len_hbm, g_hbm, x_hbm, phi_hbm, w1_hbm, w2_hbm, y_ref,
                  xg, xn, la, phi_v, pn, pnt, xs, h_v, yg, cw, qs, w1b, w2b, len_ref, g_ref,
-                 len_sem, g_sem, x_sem, phi_sem, w1_sem, w2_sem, w2l_sem,
+                 len_sem, g_sem, x_sem, phi_sem, w1_sem, w1l_sem, w2_sem, w2l_sem,
                  sx_sem, rx_sem, sy_sem, ry_sem, rl_sem):
     batch, tok, d_model = y_ref.shape
     n_exp = w1_hbm.shape[0]
@@ -75,6 +75,10 @@
 
     def w1_copy(e):
         return pltpu.make_async_copy(w1_hbm.at[e], w1b.at[lax.rem(e, ring)], w1_sem.at[lax.rem(e, ring)])
+
+    def w1_last(half):
+        cols = pl.ds(half * (ff // 2), ff // 2)
+        return pltpu.make_async_copy(w1_hbm.at[last, :, cols], w1b.at[last % ring, :, cols], w1l_sem.at[half])
 
     def w2_copy(e):
         return pltpu.make_async_copy(w2_hbm.at[e], w2b.at[lax.rem(e, ring)], w2_sem.at[lax.rem(e, ring)])
@@ -120,7 +124,9 @@
         p32 = phi_v[:, cols].astype(F32)
         pn[:, cols] = (p32 * lax.rsqrt(jnp.sum(p32 * p32, axis=0, keepdims=True) + EPSILON)).astype(BF16)
     chip_cols = pl.ds(pl.multiple_of(chip * 128, 128), 128)
-    pnt[...] = pn[:, chip_cols].T
+    half_d = d_model // 2
+    pnt[:, :half_d] = pn[:half_d, chip_cols].T
+    pnt[:, half_d:] = -pn[half_d:, chip_cols].T
     own_g.wait()
     own_len.wait()
     g = g_ref[0]
@@ -141,7 +147,9 @@
 
     def slot_logits(b, half):
         rows = xn[b, 4 * half:4 * half + 4].reshape(near_tok, d_model)
-        lt = g * lax.dot_general(own_pnt, rows, (((1,), (1,)), ((), ())), preferred_element_type=F32)
+        low, high = (lax.dot_general(own_pnt[:, d:d + half_d], rows[:, d:d + half_d], (((1,), (1,)), ((), ())),
+                                     preferred_element_type=F32) for d in (0, half_d))
+        lt = g * (low - high)
         lane = lax.broadcasted_iota(jnp.int32, lt.shape, 1)
         pos = lane
         for n, slot in enumerate(range(4 * half, 4 * half + 4)):
@@ -216,13 +224,15 @@
 
     fblk = 1024
 
-    def hidden(e, slot, negate_high=False):
+    def hidden(e, slot, split=False):
         rows = xs[:, pl.ds(pl.multiple_of(e * per, per), per), :].reshape(batch * per, d_model)
         for f in range(ff // fblk):
+            if split and f * fblk % (ff // 2) == 0:
+                w1_last(2 * f * fblk // ff).wait()
             cols = pl.ds(f * fblk, fblk)
             up = jnp.dot(rows, w1b[slot, :, cols], preferred_element_type=F32)
             act = jax.nn.gelu(up).astype(BF16).astype(F32)
-            h_v[:, cols] = -act if negate_high and f * fblk >= ff // 2 else act
+            h_v[:, cols] = -act if split and f * fblk >= ff // 2 else act
 
     def outputs(e, slot, cols):
         if cols.size > width:
@@ -234,38 +244,34 @@
         out = out.astype(BF16)
         yg[:, y_rows(me, e), cols] = out.reshape(batch, per, cols.size)
 
-    @pl.loop(0, n_exp - 1)
+    w1_copy(0).wait()
+    hidden(0, 0)
+    for half in (0, 1):
+        w1_last(half).start(priority=1)
+    w2_copy(0).wait()
+    outputs(0, 0, pl.ds(0, d_model))
+    send_own(0, pl.ds(0, d_model), ry_sem.at[0])
+    for c in range(chunks):
+        w2_last(c).start(priority=1)
+
+    @pl.loop(1, last)
     def _(e):
         w1_copy(e).wait()
         hidden(e, e)
-
-        @pl.when(e == 0)
-        def _():
-            w1_copy(last).start(priority=1)
-
         w2_copy(e).wait()
-
         for c in range(2):
             outputs(e, e, pl.ds(c * 2 * width, 2 * width))
             send_own(e, pl.ds(c * 2 * width, 2 * width), ry_sem.at[e])
 
-        @pl.when(e == 0)
-        def _():
-            for c in range(chunks):
-                w2_last(c).start(priority=1)
-
-        @pl.when(e > 1)
-        def _():
-            forward(e - 2)
-
-    w1_copy(last).wait()
+    forward(0)
     hidden(last, last % ring, True)
     for c in range(chunks):
         w2_last(c).wait()
         outputs(last, last % ring, pl.ds(c * width, width))
         send_own(last, pl.ds(c * width, width), rl_sem.at[c])
-        if c == 0:
-            forward(last - 2)
+        if c == 1:
+            for e in range(1, last - 1):
+                forward(e)
     forward(last - 1)
     for c in range(chunks):
         for rel in (1, 2, 3):
@@ -274,6 +280,15 @@
     for e in range(last):
         for rel in (0, 4, 5, 6):
             y_wait(e, rel)
+    def y_sent(rel):
+        sent = yg.at[:, pl.ds(0, slots), :]
+        pltpu.make_async_remote_copy(src_ref=sent, dst_ref=sent, send_sem=sy_sem.at[rel], recv_sem=ry_sem.at[0, rel],
+                                     device_id={"seq": part}, device_id_type=MESH).wait_send()
+
+    for copy in x_sends:
+        copy.wait_send()
+    for rel in range(4):
+        y_sent(rel)
     first = me * tok
     for c in range(chunks):
         for rel in (0, 4, 5, 6):
@@ -284,12 +299,8 @@
             pos = first + lax.broadcasted_iota(jnp.int32, mixed.shape, 0)
             y_ref[b, :, cols] = jnp.where(pos < len_ref[b], mixed, 0.0).astype(BF16)
 
-    for copy in x_sends:
-        copy.wait_send()
-    for rel in range(7):
-        sent = yg.at[:, pl.ds(0, slots), :]
-        pltpu.make_async_remote_copy(src_ref=sent, dst_ref=sent, send_sem=sy_sem.at[rel], recv_sem=ry_sem.at[0, rel],
-                                     device_id={"seq": part}, device_id_type=MESH).wait_send()
+    for rel in (4, 5, 6):
+        y_sent(rel)
 
 
 def solution(mesh):
@@ -303,7 +314,7 @@
         ring = n_exp - 1
         chunks = 4
         dma = pltpu.SemaphoreType.DMA
-        sems = (dma, dma, dma((4,)), dma, dma((ring,)), dma((ring,)), dma((chunks,)),
+        sems = (dma, dma, dma((4,)), dma, dma((ring,)), dma((2,)), dma((ring,)), dma((chunks,)),
                 dma((7, 4)), dma((7, 4)), dma((7,)), dma((n_exp, 7)), dma((chunks, 7)))
         return pl.pallas_call(
             functools.partial(layer_kernel, sems),

time: 30.5 us -> 30.3 us (level)
  no operation moved by 1% of the time
where the time goes in v6:
time: 30.3 us; the launch traced here: 30.2 us
  Pallas kernels  28.9 us (95%)
  local copies, waits for them, and re-layouts  0.66 us (2%)
  between operations  0.66 us (2%)
    pallas_call x1, Pallas kernels, local_layer(): pl.pallas_call(functools.partial(layer_kernel, sems), out_shape=pltpu.VME...  28.9 us
    unnamed x1, local copies, waits for them, and re-layouts  0.66 us

profile of v6, /device:TPU:0, one launch (start us, length us, event | category | flops | bytes accessed | tf_op | source)
XLA Modules:
  0.0 30.2 jit_solution(1523817501386656683)
XLA Ops:
  0.7 28.9 %shard_map.64 = bf16[2,32,1024]{2,1,0:T(8,128)(2,1)S(1)} custom-call(s32[2]{0:T(128)} %refs_0_.1, f32[1]{0:T(128)} %bitcast.1.refs_1_, bf16[2,32,1024]{2,1,0:T(8,128)(2,1)} %refs_2_.1, bf16[1024,512]{1,0:T(8,128)(2,1)} %refs_3_.1, bf16[4,1024,4096]{2,1,0:T(8,128)(2,1)} %refs_4_.1, bf16[4,4096,1024]{2,1,0:T(8,128)(2,1)} %refs_5_.1), custom_call_target="tpu_custom_call" | custom-call | tf_op jit(solution)/shard_map/pallas_call | solution.py:319
  29.6 0.7 %copy.8 = bf16[2,32,1024]{2,1,0:T(8,128)(2,1)} copy(bf16[2,32,1024]{2,1,0:T(8,128)(2,1)S(1)} %shard_map.64) | data formatting | bytes 262144

commit v7 on v6

--- a/solution.py
+++ b/solution.py
@@ -163,9 +163,13 @@
     for piece in (0, 1):
         x_wait(1, piece)
         x_start(2, piece, 3, ynb, 3)
+        if piece == 1:
+            x_start(2, piece, 6, ysame, 6)
         x_start(2, piece, 4, part, 4)
         x_wait(2, piece + 2)
         x_start(3, piece + 2, 3, xnb, 3)
+        if piece == 1:
+            x_start(3, piece + 2, 6, xsame, 6)
         x_start(3, piece + 2, 5, part, 5)
     for piece in range(4):
         x_wait(0, piece)
@@ -181,15 +185,16 @@
         la[b] = slot_logits(b, 0)
     for piece in (0, 2, 1, 3):
         x_wait(3, piece)
-        x_start(6, piece, 6, part, 6)
+        if piece % 2 == 0:
+            x_start(6, piece, 6, part, 6)
     for rel in (4, 5):
         for piece in range(4):
             x_wait(rel, piece)
     for slot in (4, 5, 6):
         normalise(slot)
+    for piece in range(4):
+        x_wait(6, piece)
     for b in range(batch):
-        x_wait(6, b)
-        x_wait(6, b + 2)
         xn[b, 7] = row_normed(xg[b, 7])
         near, far = la[b], slot_logits(b, 1)
         top = jnp.maximum(jnp.max(near, axis=1, keepdims=True), jnp.max(far, axis=1, keepdims=True))

time: 30.3 us -> 30.3 us (level)
  no operation moved by 1% of the time
where the time goes in v7:
time: 30.3 us; the launch traced here: 30.2 us
  Pallas kernels  28.8 us (95%)
  local copies, waits for them, and re-layouts  0.66 us (2%)
  between operations  0.66 us (2%)
    pallas_call x1, Pallas kernels, local_layer(): pl.pallas_call(functools.partial(layer_kernel, sems), out_shape=pltpu.VME...  28.8 us
    unnamed x1, local copies, waits for them, and re-layouts  0.66 us

profile of v7, /device:TPU:0, one launch (start us, length us, event | category | flops | bytes accessed | tf_op | source)
XLA Modules:
  0.0 30.2 jit_solution(13780464213564157832)
XLA Ops:
  0.7 28.8 %shard_map.64 = bf16[2,32,1024]{2,1,0:T(8,128)(2,1)S(1)} custom-call(s32[2]{0:T(128)} %refs_0_.1, f32[1]{0:T(128)} %bitcast.1.refs_1_, bf16[2,32,1024]{2,1,0:T(8,128)(2,1)} %refs_2_.1, bf16[1024,512]{1,0:T(8,128)(2,1)} %refs_3_.1, bf16[4,1024,4096]{2,1,0:T(8,128)(2,1)} %refs_4_.1, bf16[4,4096,1024]{2,1,0:T(8,128)(2,1)} %refs_5_.1), custom_call_target="tpu_custom_call" | custom-call | tf_op jit(solution)/shard_map/pallas_call | solution.py:324
  29.5 0.7 %copy.8 = bf16[2,32,1024]{2,1,0:T(8,128)(2,1)} copy(bf16[2,32,1024]{2,1,0:T(8,128)(2,1)S(1)} %shard_map.64) | data formatting | bytes 262144

commit v8 on v7

--- a/solution.py
+++ b/solution.py
@@ -115,8 +115,6 @@
     for piece in (0, 1):
         x_start(0, piece + 2, 1, xnb, 1)
         x_start(0, piece, 2, ynb, 2)
-    for piece in range(4):
-        x_start(0, piece, 0, part, 0)
 
     own_phi.wait()
     for c in range(n_slots // 128):
@@ -171,6 +169,8 @@
         if piece == 1:
             x_start(3, piece + 2, 6, xsame, 6)
         x_start(3, piece + 2, 5, part, 5)
+    for piece in range(4):
+        x_start(0, piece, 0, part, 0)
     for piece in range(4):
         x_wait(0, piece)
     normalise(1)

time: 30.3 us -> 30.3 us (level)
  no operation moved by 1% of the time
where the time goes in v8:
time: 30.3 us; the launch traced here: 30.2 us
  Pallas kernels  28.8 us (95%)
  local copies, waits for them, and re-layouts  0.66 us (2%)
  between operations  0.66 us (2%)
    pallas_call x1, Pallas kernels, local_layer(): pl.pallas_call(functools.partial(layer_kernel, sems), out_shape=pltpu.VME...  28.8 us
    unnamed x1, local copies, waits for them, and re-layouts  0.66 us

profile of v8, /device:TPU:0, one launch (start us, length us, event | category | flops | bytes accessed | tf_op | source)
XLA Modules:
  0.0 30.2 jit_solution(11799539722690952)
XLA Ops:
  0.7 28.8 %shard_map.64 = bf16[2,32,1024]{2,1,0:T(8,128)(2,1)S(1)} custom-call(s32[2]{0:T(128)} %refs_0_.1, f32[1]{0:T(128)} %bitcast.1.refs_1_, bf16[2,32,1024]{2,1,0:T(8,128)(2,1)} %refs_2_.1, bf16[1024,512]{1,0:T(8,128)(2,1)} %refs_3_.1, bf16[4,1024,4096]{2,1,0:T(8,128)(2,1)} %refs_4_.1, bf16[4,4096,1024]{2,1,0:T(8,128)(2,1)} %refs_5_.1), custom_call_target="tpu_custom_call" | custom-call | tf_op jit(solution)/shard_map/pallas_call | solution.py:324
  29.5 0.7 %copy.8 = bf16[2,32,1024]{2,1,0:T(8,128)(2,1)} copy(bf16[2,32,1024]{2,1,0:T(8,128)(2,1)S(1)} %shard_map.64) | data formatting | bytes 262144
